TPU v7x, 32 devices: a whole 2x2x4 slice. The times are simulated.
32 devices in a mesh: batch: 4 (over x, core), seq: 2 (over y), heads: 4 (over z).
Axes of the slice: x: 2, y: 2, z: 4, core: 2. Of those that a mesh axis runs over, the one named last changes fastest.
Arguments:
- hidden_in: bfloat16 [48, 5120], P('batch', 'seq'), may hold values from -7 to 7
- lengths: int32 [48], P('batch'), may hold values from 1 to 512
- draft_ids: int32 [48], P('batch'), may hold values from 0 to 31999
- input_gain: float32 [5120], P('seq'), may hold values from 0.5 to 1.5
- w_query: bfloat16 [5120, 5120], P('seq', 'heads'), may hold values from -0.078125 to 0.078125
- w_latent: bfloat16 [5120, 4, 640], P('seq', 'heads'), may hold values from -0.078125 to 0.078125
- latent_cache: bfloat16 [48, 4, 512, 640], P('batch', 'heads', 'seq'), may hold values from -1200 to 1200
- key_up: bfloat16 [4, 320, 1280], P('heads'), may hold values from -0.3125 to 0.3125
- value_up: bfloat16 [4, 320, 1280], P('heads'), may hold values from -0.3125 to 0.3125
- w_out: bfloat16 [5120, 5120], P('heads', 'seq'), may hold values from -0.078125 to 0.078125
- final_gain: float32 [5120], P('seq'), may hold values from 0.1 to 1.9
- w_vocab: bfloat16 [5120, 32000], P('seq', 'heads'), may hold values from -0.26 to 0.26
Outputs:
- new_hidden: bfloat16 [48, 5120], P('batch', 'seq')
- log_probs: float32 [48, 32000], P('batch', 'heads')
- draft_logprob: float32 [48], P('batch')
Inputs may be any that keep to these rules, and one draw needn't show every extreme that they name: `lengths`: cache positions below a request's length are its live context.
All inputs are finite; a program needn't handle non-finite values.
Results may differ from a plain program's by a relative error of at most 0.012.
The roundings to bfloat16 on the way count: a program that leaves them out, or rounds other values in their place, can miss the bound.
Values sent between devices are 32-bit elements; how exact they have to be, the bound alone decides.
No kernel may reach another device: no remote copies, remote signals or barrier semaphores. Data moves between devices by JAX's collectives and lax.ppermute only.
A program may use at most 128 MiB of HBM per device.

v0:
```python
import math
import jax
import jax.numpy as jnp
from jax import lax
from jax.sharding import PartitionSpec as P

D = 5120
HEAD_DIM = 128
GROUP_HEADS = 10
GROUP_RANK = 320
epsilon = 1e-05
negative_fill = -1e30


def merged(part, axis, combine):
    gathered = jax.tree.map(lambda a: lax.all_gather(a, axis), part)

    def take(source):
        return jax.tree.map(lambda a: lax.dynamic_index_in_dim(a, source, 0, False), gathered)

    return lax.fori_loop(
        1, lax.axis_size(axis), lambda source, state: combine(state, take(source)), take(0)
    )


def softmax_join(left_part, right_part):
    left_max, left_total, left_mixed = left_part
    right_max, right_total, right_mixed = right_part
    joined = jnp.maximum(left_max, right_max)
    left_scale = jnp.exp(left_max - joined)
    right_scale = jnp.exp(right_max - joined)
    return (
        joined,
        left_total * left_scale + right_total * right_scale,
        left_mixed * left_scale[..., None] + right_mixed * right_scale[..., None],
    )


def vocab_join(left_part, right_part):
    left_max, left_total, left_pick = left_part
    right_max, right_total, right_pick = right_part
    joined = jnp.maximum(left_max, right_max)
    return (
        joined,
        left_total * jnp.exp(left_max - joined) + right_total * jnp.exp(right_max - joined),
        left_pick + right_pick,
    )


def vocab_stats(logits, columns, draft_ids):
    picked_local = jnp.sum(jnp.where(columns[None, :] == draft_ids[:, None], logits, 0.0), axis=1)
    local_top = jnp.max(logits, axis=1)
    return (picked_local, local_top)


def body(
    hidden_in,
    lengths,
    draft_ids,
    input_gain,
    w_query,
    w_latent,
    latent_cache,
    key_up,
    value_up,
    w_out,
    final_gain,
    w_vocab,
):
    batch_rows = hidden_in.shape[0]
    scaling = 1.0 / math.sqrt(HEAD_DIM)
    highest_prec = lax.Precision.HIGHEST
    states = hidden_in.astype(jnp.float32)
    gained = (states * input_gain).astype(jnp.bfloat16)
    query_part = jnp.dot(gained, w_query, preferred_element_type=jnp.float32)
    latent_matrix = w_latent.reshape(w_latent.shape[0], 2 * GROUP_RANK)
    latent_part = jnp.dot(gained, latent_matrix, preferred_element_type=jnp.float32)
    square_part = jnp.sum(states * states, axis=1)
    query_sum, latent_sum, square_sum = lax.psum((query_part, latent_part, square_part), "seq")
    inv_rms = lax.rsqrt(square_sum / D + epsilon)[:, None]
    query_rows = (inv_rms * query_sum).astype(jnp.bfloat16)
    latent = (inv_rms * latent_sum).astype(jnp.bfloat16)
    key_table = key_up[0].reshape(GROUP_RANK, GROUP_HEADS, HEAD_DIM)
    absorbed = jnp.einsum(
        "bhd,rhd->bhr",
        query_rows.reshape(batch_rows, GROUP_HEADS, HEAD_DIM),
        key_table,
        preferred_element_type=jnp.float32,
    ).astype(jnp.bfloat16)
    cache_rows = latent_cache[:, 0]
    local_span = cache_rows.shape[1]
    scores = (
        jnp.einsum(
            "bhr,btr->bht",
            absorbed,
            cache_rows[:, :, :GROUP_RANK],
            preferred_element_type=jnp.float32,
        )
        * scaling
    )
    positions = lax.axis_index("seq") * local_span + jnp.arange(local_span, dtype=jnp.int32)
    live_mask = positions[None, None, :] < lengths[:, None, None]
    scores = jnp.where(live_mask, scores, negative_fill)
    local_max = jnp.max(scores, axis=2)
    weights = jnp.where(live_mask, jnp.exp(scores - local_max[..., None]), 0.0)
    local_total = jnp.sum(weights, axis=2)
    local_mixed = jnp.einsum(
        "bht,btr->bhr",
        weights.astype(jnp.bfloat16),
        cache_rows[:, :, GROUP_RANK:],
        preferred_element_type=jnp.float32,
    )
    own_score = (
        jnp.einsum(
            "bhr,br->bh", absorbed, latent[:, :GROUP_RANK], preferred_element_type=jnp.float32
        )
        * scaling
    )
    own_value = latent[:, None, GROUP_RANK:].astype(jnp.float32)
    value_table = value_up[0].astype(jnp.float32).reshape(GROUP_RANK, GROUP_HEADS, HEAD_DIM)
    merged_max, merged_total, merged_mixed = merged(
        (local_max, local_total, local_mixed), "seq", softmax_join
    )
    highest = jnp.maximum(merged_max, own_score)
    cache_scale = jnp.exp(merged_max - highest)
    own_weight = jnp.exp(own_score - highest)
    denominator = merged_total * cache_scale + own_weight
    mixed_sum = merged_mixed * cache_scale[..., None] + own_weight[..., None] * own_value
    latent_out = mixed_sum / denominator[..., None]
    head_out = jnp.einsum("bhr,rhd->bhd", latent_out, value_table, precision=highest_prec).astype(
        jnp.bfloat16
    )
    head_out = head_out.reshape(batch_rows, GROUP_HEADS * HEAD_DIM)
    attn_part = jnp.dot(head_out, w_out, preferred_element_type=jnp.float32)
    attn_sum = lax.psum(attn_part, "heads")
    updated = states + attn_sum
    new_hidden = updated.astype(jnp.bfloat16)
    final_terms = jnp.dot(
        (updated * final_gain).astype(jnp.bfloat16), w_vocab, preferred_element_type=jnp.float32
    )
    final_squares = jnp.sum(updated * updated, axis=1)
    vocab_width = w_vocab.shape[1]
    vocab_start = lax.axis_index("heads") * vocab_width
    logit_sum, square_total = lax.psum((final_terms, final_squares), "seq")
    logits = lax.rsqrt(square_total / D + epsilon)[:, None] * logit_sum
    columns = vocab_start + jnp.arange(vocab_width, dtype=jnp.int32)
    picked_local, local_top = vocab_stats(logits, columns, draft_ids)
    local_sum = jnp.sum(jnp.exp(logits - local_top[:, None]), axis=1)
    top_all, total_all, picked = merged((local_top, local_sum, picked_local), "heads", vocab_join)
    log_total = top_all + jnp.log(total_all)
    log_probs = logits - log_total[:, None]
    draft_logprob = picked - log_total
    return (new_hidden, log_probs, draft_logprob)


def solution(mesh):
    return jax.shard_map(
        body,
        mesh=mesh,
        in_specs=(
            P("batch", "seq"),
            P("batch"),
            P("batch"),
            P("seq"),
            P("seq", "heads"),
            P("seq", "heads", None),
            P("batch", "heads", "seq", None),
            P("heads", None, None),
            P("heads", None, None),
            P("heads", "seq"),
            P("seq"),
            P("seq", "heads"),
        ),
        out_specs=(P("batch", "seq"), P("batch", "heads"), P("batch")),
        check_vma=False,
    )
```

profile of v0, /device:TPU:0, one launch (start us, length us, event | category | flops | bytes accessed | tf_op | source)
XLA Modules:
  0.0 174.1 jit_solution(14055392007863681934)
XLA Ops:
  7.2 0.0 copy-start
  7.2 0.0 all-reduce.13.cloned.1.call-start
  7.3 1.7 fusion.26
  8.9 4.5 %fusion.40 = f32[12,1280]{1,0:T(8,128)} fusion(bf16[2560,1280]{1,0:T(8,128)(2,1)} %param.18, bf16[12,2560]{1,0:T(8,128)(2,1)} %param.14, f32[2560]{0:T(1024)} %param.17), kind=kOutput, calls=%fused_computation.52 | convolution fusion | flops 78735360 | bytes 6686720 | tf_op jit(solution)/shard_map/dot_general | solution.py:75
  13.5 1.2 fusion.7
  14.6 0.0 all-reduce.13.cloned.1.call-update
  14.7 0.0 all-reduce.9.cloned.1.call-start
  14.7 0.1 broadcast_compare_fusion
  14.8 1.6 copy.30
  16.4 6.4 %copy.33 = bf16[12,1,256,640]{2,3,0,1:T(8,128)(2,1)} copy(bf16[12,1,256,640]{3,2,1,0:T(8,128)(2,1)} %param.20) | data formatting | bytes 7864320 | tf_op args[6]
  22.7 0.6 copy.35
  23.4 15.8 %all-reduce.13.cloned.1.call-done = (f32[12,1280]{1,0:T(8,128)}, f32[12]{0:T(128)}, f32[12,640]{1,0:T(8,128)}) async-done(((f32[12,1280]{1,0:T(8,128)}, f32[12]{0:T(128)}, f32[12,640]{1,0:T(8,128)}), (f32[12,1280]{1,0:T(8,128)}, f32[12]{0:T(128)}, f32[12,640]{1,0:T(8,128)})) %all-reduce.13.cloned.1.call-update) | async-done | bytes 92224 | tf_op jit(solution)/shard_map/psum | solution.py:79
  39.2 0.7 add_rsqrt_fusion.1
  39.9 1.0 multiply_convert_fusion.2
  40.9 0.3 fusion.19
  41.2 2.0 %fusion.58 = (f32[12,10]{1,0:T(8,128)S(1)}, f32[12,10,256]{2,1,0:T(8,128)S(1)}) fusion(bf16[12,256,640]{1,2,0:T(8,128)(2,1)} %bitcast.84, bf16[12,10,320]{2,0,1:T(8,128)(2,1)S(1)} %fusion.19, pred[12,256]{1,0:T(8,128)(4,1)S(1)} %broadcast_compare_fusion), kind=kOutput, calls=%fused_computation.84 | convolution fusion | flops 19752840 | bytes 2169312 | tf_op jit(solution)/shard_map/bhr,btr->bht/dot_general | solution.py:93
  43.2 0.2 fusion.28
  43.4 2.2 %fusion.9 = f32[12,10,320]{2,1,0:T(8,128)S(1)} fusion(bf16[12,256,640]{1,2,0:T(8,128)(2,1)} %bitcast.85, f32[12,10,256]{2,1,0:T(8,128)S(1)} %get-tuple-element.245, f32[12,10]{1,0:T(8,128)S(1)} %get-tuple-element.244, pred[12,256]{1,0:T(8,128)(4,1)S(1)} %broadcast_compare_fusion), kind=kOutput, calls=%fused_computation.12 | convolution fusion | flops 19752960 | bytes 2246112 | tf_op jit(solution)/shard_map/bht,btr->bhr/dot_general | solution.py:107
  45.6 4.4 %all-gather.7 = f32[2,12,10]{2,1,0:T(8,128)S(1)} all-gather(f32[1,12,10]{2,1,0:T(8,128)S(1)} %bitcast.91), channel_id=4, replica_groups=mesh['batch'=4,'seq'=2,'heads'=4] {'seq'}, dimensions={0}, use_global_device_ids=true | all-gather | bytes 1440 | tf_op jit(solution)/shard_map/all_gather | solution.py:16
  50.0 4.3 %all-gather.6 = f32[2,12,10]{2,1,0:T(8,128)S(1)} all-gather(f32[1,12,10]{2,1,0:T(8,128)S(1)} %bitcast.90), channel_id=3, replica_groups=mesh['batch'=4,'seq'=2,'heads'=4] {'seq'}, dimensions={0}, use_global_device_ids=true | all-gather | bytes 1440 | tf_op jit(solution)/shard_map/all_gather | solution.py:16
  54.3 0.1 multiply_convert_fusion.3
  54.4 0.1 slice_convert_fusion
  54.5 0.2 fusion.30
  54.7 7.4 %all-gather = f32[24,10,320]{2,1,0:T(8,128)S(1)} all-gather(f32[12,10,320]{2,1,0:T(8,128)S(1)} %fusion.9), channel_id=2, replica_groups=mesh['batch'=4,'seq'=2,'heads'=4] {'seq'}, dimensions={0}, use_global_device_ids=true | all-gather | bytes 460800 | tf_op jit(solution)/shard_map/all_gather | solution.py:16
  62.1 0.2 fusion.24
  62.3 1.1 fusion.20
  63.5 4.5 %fusion.59 = f32[12,2560]{1,0:T(8,128)} fusion(bf16[12,1280]{1,0:T(8,128)(2,1)S(1)} %bitcast.89, bf16[1280,2560]{1,0:T(8,128)(2,1)} %param.23), kind=kOutput, calls=%fused_computation.85 | convolution fusion | flops 78643200 | bytes 6707200 | tf_op jit(solution)/shard_map/dot_general | solution.py:134
  68.0 0.0 all-reduce.9.cloned.1.call-update
  68.0 0.0 all-reduce.11.cloned.1.call-start
  68.1 0.6 dynamic-slice
  69.3 33.7 %all-reduce.9.cloned.1.call-done = f32[12,2560]{1,0:T(8,128)} async-done(((f32[12,2560]{1,0:T(8,128)}), f32[12,2560]{1,0:T(8,128)}) %all-reduce.9.cloned.1.call-update) | async-done | bytes 122896 | tf_op jit(solution)/shard_map/psum | solution.py:135
  103.1 18.3 %fusion.37 = f32[12,8000]{1,0:T(8,128)} fusion(bf16[2560,8000]{0,1:T(8,128)(2,1)} %param.25, f32[2560]{0:T(1024)} %param.24, f32[12,2560]{1,0:T(8,128)} %all-reduce.9.cloned.1.call-done, bf16[12,2560]{1,0:T(8,128)(2,1)S(1)} %copy-done.2), kind=kOutput, calls=%fused_computation.49 | convolution fusion | flops 491642880 | bytes 41538560 | tf_op jit(solution)/shard_map/dot_general | solution.py:138
  121.4 0.0 all-reduce.11.cloned.1.call-update
  121.4 1.3 multiply_reduce_fusion.1
  122.7 5.0 %psum.46 = f32[12]{0:T(128)S(1)} all-reduce(f32[12]{0:T(128)} %get-tuple-element.240), channel_id=1, replica_groups=mesh['batch'=4,'seq'=2,'heads'=4] {'seq'}, use_global_device_ids=true, to_apply=%region_8.9 | all-reduce | flops 12 | bytes 96 | tf_op jit(solution)/shard_map/psum | solution.py:144
  127.7 22.0 %all-reduce.11.cloned.1.call-done = f32[12,8000]{1,0:T(8,128)} async-done(((f32[12,8000]{1,0:T(8,128)}), f32[12,8000]{1,0:T(8,128)}) %all-reduce.11.cloned.1.call-update) | async-done | bytes 384016 | tf_op jit(solution)/shard_map/psum | solution.py:144
  149.7 1.3 multiply_reduce_fusion
  151.0 0.2 dynamic-update-slice
  151.2 1.4 select_reduce_fusion
  152.6 0.2 dynamic-update-slice.2
  152.8 0.2 dynamic-update-slice.1
  153.1 11.7 %all-reduce.3 = (f32[48]{0:T(128)S(1)}, f32[48]{0:T(128)S(1)}, f32[48]{0:T(128)S(1)}) all-reduce(f32[48]{0:T(128)S(1)} %dynamic-update-slice, f32[48]{0:T(128)S(1)} %dynamic-update-slice.1, f32[48]{0:T(128)S(1)} %dynamic-update-slice.2), channel_id=5, replica_groups=mesh['batch'=4,'seq'=2,'heads'=4] {'heads'}, use_global_device_ids=true, to_apply=%add | all-reduce | flops 144 | bytes 1152
  164.7 0.1 reshape.101
  164.8 0.1 reshape.102
  164.9 0.1 reshape.103
  165.0 0.1 while.12
  165.1 0.5 fusion.55
  165.6 1.9 %multiply_subtract_fusion = f32[12,8000]{1,0:T(8,128)} fusion(f32[12,8000]{1,0:T(8,128)} %all-reduce.11.cloned.1.call-done, f32[12]{0:T(128)S(1)} %get-tuple-element.233, f32[12]{0:T(128)S(1)} %add_rsqrt_fusion), kind=kLoop, calls=%fused_computation.24 | loop fusion | flops 192000 | bytes 768096 | tf_op jit(solution)/shard_map/sub | solution.py:151
  (31 shorter events, 0.3 us)
Async XLA Ops:
  7.2 6.3 %copy-start = (bf16[2560,1,640]{2,0,1:T(8,128)(2,1)S(1)}, bf16[2560,1,640]{2,0,1:T(8,128)(2,1)}, u32[]{:S(2)}) copy-start(bf16[2560,1,640]{2,0,1:T(8,128)(2,1)} %param.19) | copy-start | bytes 9830404
  7.2 6.3 %copy-start.2 = (bf16[12,2560]{1,0:T(8,128)(2,1)S(1)}, bf16[12,2560]{1,0:T(8,128)(2,1)}, u32[]{:S(2)}) copy-start(bf16[12,2560]{1,0:T(8,128)(2,1)} %param.14) | copy-start | bytes 184324
  7.2 6.3 %copy-start.5 = (f32[2560]{0:T(1024)S(1)}, f32[2560]{0:T(1024)}, u32[]{:S(2)}) copy-start(f32[2560]{0:T(1024)} %param.17) | copy-start | bytes 30724
  7.2 32.0 %all-reduce.13.cloned.1.call-start = ((), (), s32[]{:S(2)}) async-start(), calls=%async_computation.2 | async-start | bytes 246784 | tf_op jit(solution)/shard_map/psum | solution.py:79
  8.9 5.8 %copy-start.7 = (s32[12]{0:T(128)S(1)}, s32[12]{0:T(128)}, u32[]{:S(2)}) copy-start(s32[12]{0:T(128)} %param.15) | copy-start | bytes 148
  14.7 88.4 %all-reduce.9.cloned.1.call-start = ((), (), s32[]{:S(2)}) async-start(), calls=%async_computation | async-start | bytes 327680 | tf_op jit(solution)/shard_map/psum | solution.py:135
  16.4 6.4 %copy-start.4 = (bf16[1,320,1280]{2,1,0:T(8,128)(2,1)S(1)}, bf16[1,320,1280]{2,1,0:T(8,128)(2,1)}, u32[]{:S(2)}) copy-start(bf16[1,320,1280]{2,1,0:T(8,128)(2,1)} %param.22) | copy-start | bytes 2457604
  39.2 15.2 %copy-start.6 = (f32[12,640]{1,0:T(8,128)S(1)}, f32[12,640]{1,0:T(8,128)}, u32[]{:S(2)}) copy-start(f32[12,640]{1,0:T(8,128)} %get-tuple-element.229) | copy-start | bytes 92164
  63.4 4.7 %copy-start.8 = (u32[32]{0:T(128)S(1)}, u32[32]{0:T(128)}, u32[]{:S(2)}) copy-start(u32[32]{0:T(128)} %constant.107) | copy-start | bytes 388
  68.0 81.7 %all-reduce.11.cloned.1.call-start = ((), (), s32[]{:S(2)}) async-start(), calls=%async_computation.1 | async-start | bytes 1032192 | tf_op jit(solution)/shard_map/psum | solution.py:144
  103.0 18.3 %copy-start.3 = (f32[12,2560]{1,0:T(8,128)S(1)}, f32[12,2560]{1,0:T(8,128)}, u32[]{:S(2)}) copy-start(f32[12,2560]{1,0:T(8,128)} %all-reduce.9.cloned.1.call-done) | copy-start | bytes 368644
  103.0 64.5 %copy-start.1 = (bf16[2560,1,640]{2,0,1:T(8,128)(2,1)S(1)}, bf16[2560,1,640]{2,0,1:T(8,128)(2,1)}, u32[]{:S(2)}) copy-start(bf16[2560,1,640]{2,0,1:T(8,128)(2,1)} %param.19) | copy-start | bytes 9830404
Sparse Core Ops, SparseCore 0:
  14.8 24.3 all-reduce.12
  68.1 34.8 all-reduce.8
  121.5 28.1 all-reduce.10
where the time goes:
time: 175 us; the launch traced here: 174 us
  waiting for transfers between devices  71.6 us (41%)
  matrix products  34.3 us (20%)
  blocking collectives  32.8 us (19%)
  between operations  14.6 us (8%)
  other arithmetic  10.5 us (6%)
  local copies, waits for them, and re-layouts  10.2 us (6%)
    psum x1, waiting for transfers between devices, body(): attn_sum = lax.psum(attn_part, 'heads')  33.7 us
    psum x1, waiting for transfers between devices, body(): logit_sum, square_total = lax.psum((final_terms, final_squares), 'seq')  22 us
    dot_general x1, matrix products, body(): jnp.dot((updated * final_gain).astype(jnp.bfloat16), w_vocab, preferred_e...  18.3 us
    all_gather x3, blocking collectives, merged(): gathered = jax.tree.map(lambda a: lax.all_gather(a, axis), part)  16.1 us
    psum x1, waiting for transfers between devices, body(): lax.psum((query_part, latent_part, square_part), 'seq')  15.8 us
    unnamed x1, blocking collectives  11.7 us
    unnamed x30, local copies, waits for them, and re-layouts  9.88 us
    psum x1, blocking collectives, body(): logit_sum, square_total = lax.psum((final_terms, final_squares), 'seq')  5.04 us
  transfers between devices with their start and end apart: 3, of which 3 were waited for; matrix products, arithmetic and copies ran while one was open for 6% of the time, Pallas kernels for 0%

commit v1 on v0

--- a/solution.py
+++ b/solution.py
@@ -132,7 +132,7 @@
     )
     head_out = head_out.reshape(batch_rows, GROUP_HEADS * HEAD_DIM)
     attn_part = jnp.dot(head_out, w_out, preferred_element_type=jnp.float32)
-    attn_sum = lax.psum(attn_part, "heads")
+    attn_sum = jnp.sum(lax.all_gather(attn_part, "heads"), axis=0)
     updated = states + attn_sum
     new_hidden = updated.astype(jnp.bfloat16)
     final_terms = jnp.dot(

time: 175 us -> 156 us (0.89)
  waiting for transfers between devices: 71.6 us -> 36.6 us
  blocking collectives: 32.8 us -> 49.5 us
    psum x1 -> x0, waiting for transfers between devices: 33.7 us -> none  [body(): attn_sum = lax.psum(attn_part, 'heads')]
    all_gather x0 -> x1, blocking collectives: none -> 16.7 us  [body(): attn_sum = jnp.sum(lax.all_gather(attn_part, 'heads'), axis=0)]
    unnamed x30 -> x28, local copies, waits for them, and re-layouts: 9.88 us -> 9.85 us
  transfers between devices with their start and end apart: 3 -> 2, of which waited for: 3 -> 2; matrix products, arithmetic and copies ran while one was open for 6% -> 7% of each run, Pallas kernels for 0% -> 0%
where the time goes in v1:
time: 156 us; the launch traced here: 155 us
  blocking collectives  49.5 us (32%)
  waiting for transfers between devices  36.6 us (23%)
  matrix products  33.7 us (22%)
  between operations  14.8 us (9%)
  other arithmetic  10.5 us (7%)
  local copies, waits for them, and re-layouts  10.2 us (7%)
    psum x1, waiting for transfers between devices, body(): logit_sum, square_total = lax.psum((final_terms, final_squares), 'seq')  21.9 us
    dot_general x1, matrix products, body(): jnp.dot((updated * final_gain).astype(jnp.bfloat16), w_vocab, preferred_e...  18.4 us
    all_gather x1, blocking collectives, body(): attn_sum = jnp.sum(lax.all_gather(attn_part, 'heads'), axis=0)  16.7 us
    all_gather x3, blocking collectives, merged(): gathered = jax.tree.map(lambda a: lax.all_gather(a, axis), part)  16.1 us
    psum x1, waiting for transfers between devices, body(): lax.psum((query_part, latent_part, square_part), 'seq')  14.6 us
    unnamed x1, blocking collectives  11.7 us
    unnamed x28, local copies, waits for them, and re-layouts  9.85 us
    psum x1, blocking collectives, body(): logit_sum, square_total = lax.psum((final_terms, final_squares), 'seq')  5.04 us
  transfers between devices with their start and end apart: 2, of which 2 were waited for; matrix products, arithmetic and copies ran while one was open for 7% of the time, Pallas kernels for 0%

profile of v1, /device:TPU:0, one launch (start us, length us, event | category | flops | bytes accessed | tf_op | source)
XLA Modules:
  0.0 155.3 jit_solution(11653465097052662246)
XLA Ops:
  7.2 0.0 copy-start
  7.2 0.0 copy-start.2
  7.2 0.0 all-reduce.10.cloned.1.call-start
  7.3 1.7 %fusion.26 = f32[12]{0:T(128)} fusion(bf16[12,2560]{1,0:T(8,128)(2,1)} %param.14), kind=kLoop, calls=%fused_computation.38 | loop fusion | flops 92148 | bytes 61488 | tf_op jit(solution)/shard_map/reduce_sum | solution.py:78
  8.9 4.5 %fusion.40 = f32[12,1280]{1,0:T(8,128)} fusion(bf16[2560,1280]{1,0:T(8,128)(2,1)} %param.18, bf16[12,2560]{1,0:T(8,128)(2,1)} %param.14, f32[2560]{0:T(1024)} %param.17), kind=kOutput, calls=%fused_computation.53 | convolution fusion | flops 78735360 | bytes 6686720 | tf_op jit(solution)/shard_map/dot_general | solution.py:75
  13.5 1.2 fusion.7
  14.6 0.0 all-reduce.10.cloned.1.call-update
  14.7 0.0 all-reduce.8.cloned.1.call-start
  14.7 1.6 %copy.30 = bf16[1,320,1280]{1,2,0:T(8,128)(2,1)S(1)} copy(bf16[1,320,1280]{2,1,0:T(8,128)(2,1)} %param.21) | data formatting | bytes 1638400 | tf_op args[7]
  16.3 0.0 copy-start.7
  16.3 6.3 %copy.33 = bf16[12,1,256,640]{2,3,0,1:T(8,128)(2,1)} copy(bf16[12,1,256,640]{3,2,1,0:T(8,128)(2,1)} %param.20) | data formatting | bytes 7864320 | tf_op args[6]
  22.7 0.6 copy.35
  23.3 0.1 broadcast_compare_fusion
  23.4 0.6 dynamic-slice
  24.5 14.6 %all-reduce.10.cloned.1.call-done = (f32[12,1280]{1,0:T(8,128)}, f32[12]{0:T(128)}, f32[12,640]{1,0:T(8,128)}) async-done(((f32[12,1280]{1,0:T(8,128)}, f32[12]{0:T(128)}, f32[12,640]{1,0:T(8,128)}), (f32[12,1280]{1,0:T(8,128)}, f32[12]{0:T(128)}, f32[12,640]{1,0:T(8,128)})) %all-reduce.10.cloned.1.call-update) | async-done | bytes 92224 | tf_op jit(solution)/shard_map/psum | solution.py:79
  39.2 0.6 add_rsqrt_fusion.1
  39.8 1.0 multiply_convert_fusion.2
  40.8 0.3 fusion.19
  41.1 2.0 %fusion.58 = (f32[12,10]{1,0:T(8,128)S(1)}, f32[12,10,256]{2,1,0:T(8,128)S(1)}) fusion(bf16[12,256,640]{1,2,0:T(8,128)(2,1)} %bitcast.86, bf16[12,10,320]{2,0,1:T(8,128)(2,1)S(1)} %fusion.19, pred[12,256]{1,0:T(8,128)(4,1)S(1)} %broadcast_compare_fusion), kind=kOutput, calls=%fused_computation.85 | convolution fusion | flops 19752840 | bytes 2169312 | tf_op jit(solution)/shard_map/bhr,btr->bht/dot_general | solution.py:93
  43.1 0.2 fusion.28
  43.3 2.2 %fusion.9 = f32[12,10,320]{2,1,0:T(8,128)S(1)} fusion(bf16[12,256,640]{1,2,0:T(8,128)(2,1)} %bitcast.87, f32[12,10,256]{2,1,0:T(8,128)S(1)} %get-tuple-element.245, f32[12,10]{1,0:T(8,128)S(1)} %get-tuple-element.244, pred[12,256]{1,0:T(8,128)(4,1)S(1)} %broadcast_compare_fusion), kind=kOutput, calls=%fused_computation.13 | convolution fusion | flops 19752960 | bytes 2246112 | tf_op jit(solution)/shard_map/bht,btr->bhr/dot_general | solution.py:107
  45.6 4.4 %all-gather.8 = f32[2,12,10]{2,1,0:T(8,128)S(1)} all-gather(f32[1,12,10]{2,1,0:T(8,128)S(1)} %bitcast.93), channel_id=4, replica_groups=mesh['batch'=4,'seq'=2,'heads'=4] {'seq'}, dimensions={0}, use_global_device_ids=true | all-gather | bytes 1440 | tf_op jit(solution)/shard_map/all_gather | solution.py:16
  49.9 4.3 %all-gather.7 = f32[2,12,10]{2,1,0:T(8,128)S(1)} all-gather(f32[1,12,10]{2,1,0:T(8,128)S(1)} %bitcast.92), channel_id=3, replica_groups=mesh['batch'=4,'seq'=2,'heads'=4] {'seq'}, dimensions={0}, use_global_device_ids=true | all-gather | bytes 1440 | tf_op jit(solution)/shard_map/all_gather | solution.py:16
  54.3 0.1 multiply_convert_fusion.3
  54.4 0.1 slice_convert_fusion
  54.4 0.2 fusion.30
  54.6 7.4 %all-gather = f32[24,10,320]{2,1,0:T(8,128)S(1)} all-gather(f32[12,10,320]{2,1,0:T(8,128)S(1)} %fusion.9), channel_id=2, replica_groups=mesh['batch'=4,'seq'=2,'heads'=4] {'seq'}, dimensions={0}, use_global_device_ids=true | all-gather | bytes 460800 | tf_op jit(solution)/shard_map/all_gather | solution.py:16
  62.0 0.2 fusion.24
  62.2 1.1 fusion.20
  63.4 3.8 %convolution_bitcast_fusion = f32[1,12,2560]{2,1,0:T(8,128)S(1)} fusion(bf16[12,1280]{1,0:T(8,128)(2,1)S(1)} %bitcast.91, bf16[1280,2560]{1,0:T(8,128)(2,1)} %param.23), kind=kOutput, calls=%fused_computation.10 | convolution fusion | flops 78643200 | bytes 6707200 | tf_op jit(solution)/shard_map/dot_general | solution.py:134
  67.2 16.7 %all-gather.9 = f32[4,12,2560]{2,1,0:T(8,128)S(1)} all-gather(f32[1,12,2560]{2,1,0:T(8,128)S(1)} %convolution_bitcast_fusion), channel_id=5, replica_groups=mesh['batch'=4,'seq'=2,'heads'=4] {'heads'}, dimensions={0}, use_global_device_ids=true | all-gather | bytes 614400 | tf_op jit(solution)/shard_map/all_gather | solution.py:135
  84.0 18.4 %fusion.37 = f32[12,8000]{1,0:T(8,128)} fusion(bf16[2560,8000]{0,1:T(8,128)(2,1)} %param.25, f32[2560]{0:T(1024)} %param.24, f32[12,2560]{1,0:T(8,128)S(1)} %reduce_sum.56, bf16[12,2560]{1,0:T(8,128)(2,1)S(1)} %copy-done.2), kind=kOutput, calls=%fused_computation.50 | convolution fusion | flops 491642880 | bytes 41538560 | tf_op jit(solution)/shard_map/dot_general | solution.py:138
  102.4 0.0 all-reduce.8.cloned.1.call-update
  102.4 1.3 multiply_reduce_fusion.1
  103.7 5.0 %psum.38 = f32[12]{0:T(128)S(1)} all-reduce(f32[12]{0:T(128)} %get-tuple-element.240), channel_id=1, replica_groups=mesh['batch'=4,'seq'=2,'heads'=4] {'seq'}, use_global_device_ids=true, to_apply=%region_8.9 | all-reduce | flops 12 | bytes 96 | tf_op jit(solution)/shard_map/psum | solution.py:144
  108.7 21.9 %all-reduce.8.cloned.1.call-done = f32[12,8000]{1,0:T(8,128)} async-done(((f32[12,8000]{1,0:T(8,128)}), f32[12,8000]{1,0:T(8,128)}) %all-reduce.8.cloned.1.call-update) | async-done | bytes 384016 | tf_op jit(solution)/shard_map/psum | solution.py:144
  130.6 1.3 multiply_reduce_fusion
  131.9 0.2 dynamic-update-slice
  132.2 1.4 select_reduce_fusion
  133.6 0.2 dynamic-update-slice.2
  133.8 0.2 dynamic-update-slice.1
  134.0 11.7 %all-reduce.3 = (f32[48]{0:T(128)S(1)}, f32[48]{0:T(128)S(1)}, f32[48]{0:T(128)S(1)}) all-reduce(f32[48]{0:T(128)S(1)} %dynamic-update-slice, f32[48]{0:T(128)S(1)} %dynamic-update-slice.1, f32[48]{0:T(128)S(1)} %dynamic-update-slice.2), channel_id=6, replica_groups=mesh['batch'=4,'seq'=2,'heads'=4] {'heads'}, use_global_device_ids=true, to_apply=%add | all-reduce | flops 144 | bytes 1152
  145.7 0.1 reshape.102
  145.7 0.1 reshape.103
  145.8 0.1 reshape.104
  145.9 0.1 while.12
  146.0 0.5 fusion.55
  146.6 1.9 %multiply_subtract_fusion = f32[12,8000]{1,0:T(8,128)} fusion(f32[12,8000]{1,0:T(8,128)} %all-reduce.8.cloned.1.call-done, f32[12]{0:T(128)S(1)} %get-tuple-element.233, f32[12]{0:T(128)S(1)} %add_rsqrt_fusion), kind=kLoop, calls=%fused_computation.25 | loop fusion | flops 192000 | bytes 768096 | tf_op jit(solution)/shard_map/sub | solution.py:151
  (28 shorter events, 0.3 us)
Async XLA Ops:
  7.2 6.3 %copy-start = (bf16[2560,1,640]{2,0,1:T(8,128)(2,1)S(1)}, bf16[2560,1,640]{2,0,1:T(8,128)(2,1)}, u32[]{:S(2)}) copy-start(bf16[2560,1,640]{2,0,1:T(8,128)(2,1)} %param.19) | copy-start | bytes 9830404
  7.2 6.3 %copy-start.2 = (bf16[12,2560]{1,0:T(8,128)(2,1)S(1)}, bf16[12,2560]{1,0:T(8,128)(2,1)}, u32[]{:S(2)}) copy-start(bf16[12,2560]{1,0:T(8,128)(2,1)} %param.14) | copy-start | bytes 184324
  7.2 6.3 %copy-start.4 = (f32[2560]{0:T(1024)S(1)}, f32[2560]{0:T(1024)}, u32[]{:S(2)}) copy-start(f32[2560]{0:T(1024)} %param.17) | copy-start | bytes 30724
  7.2 32.0 %all-reduce.10.cloned.1.call-start = ((), (), s32[]{:S(2)}) async-start(), calls=%async_computation.1 | async-start | bytes 246784 | tf_op jit(solution)/shard_map/psum | solution.py:79
  14.7 116.0 %all-reduce.8.cloned.1.call-start = ((), (), s32[]{:S(2)}) async-start(), calls=%async_computation | async-start | bytes 1032192 | tf_op jit(solution)/shard_map/psum | solution.py:144
  16.3 6.4 %copy-start.3 = (bf16[1,320,1280]{2,1,0:T(8,128)(2,1)S(1)}, bf16[1,320,1280]{2,1,0:T(8,128)(2,1)}, u32[]{:S(2)}) copy-start(bf16[1,320,1280]{2,1,0:T(8,128)(2,1)} %param.22) | copy-start | bytes 2457604
  16.3 7.0 %copy-start.6 = (s32[12]{0:T(128)S(1)}, s32[12]{0:T(128)}, u32[]{:S(2)}) copy-start(s32[12]{0:T(128)} %param.15) | copy-start | bytes 148
  16.3 7.1 %copy-start.7 = (u32[32]{0:T(128)S(1)}, u32[32]{0:T(128)}, u32[]{:S(2)}) copy-start(u32[32]{0:T(128)} %constant.107) | copy-start | bytes 388
  39.2 15.1 %copy-start.5 = (f32[12,640]{1,0:T(8,128)S(1)}, f32[12,640]{1,0:T(8,128)}, u32[]{:S(2)}) copy-start(f32[12,640]{1,0:T(8,128)} %get-tuple-element.229) | copy-start | bytes 92164
  84.0 64.5 %copy-start.1 = (bf16[2560,1,640]{2,0,1:T(8,128)(2,1)S(1)}, bf16[2560,1,640]{2,0,1:T(8,128)(2,1)}, u32[]{:S(2)}) copy-start(bf16[2560,1,640]{2,0,1:T(8,128)(2,1)} %param.19) | copy-start | bytes 9830404
Sparse Core Ops, SparseCore 0:
  14.8 24.3 all-reduce.9
  102.5 28.0 all-reduce.7
